TPU v7x, 128 devices: a whole 4x4x4 slice. The times are simulated.
128 devices in a mesh: batch: 8 (over z, core), seq: 16 (over x, y).
Axes of the slice: x: 4, y: 4, z: 4, core: 2. Of those that a mesh axis runs over, the one named last changes fastest.
Arguments:
- queries: bfloat16 [65536, 8, 256], P(('batch', 'seq')), parts along dimension 0, may hold values from -400 to 400
- key_heads: bfloat16 [65536, 4, 256], P(('batch', 'seq')), parts along dimension 0, may hold values from -16 to 16
- projected_value_heads: bfloat16 [65536, 4, 256], P(('batch', 'seq')), parts along dimension 0, may hold values from -6 to 6
- lengths: int32 [8], P('batch'), parts along dimension 0, may hold values from 7681 to 8192
Outputs:
- attended: bfloat16 [65536, 8, 256], P(('batch', 'seq')), parts along dimension 0
There are 8 independent parts, one for each index of `batch`. A program takes and returns all parts, laid end to end along the dimension named above; each array names one. Nothing has to cross between parts.
All inputs are finite; a program needn't handle non-finite values.
Results may differ from a plain program's by a relative error of at most 0.0033.
Values may be sent and summed in bfloat16 or wider, within the bound.
A program may use at most 192 MiB of HBM per device.

v0:
```python
import math
import jax
import jax.numpy as jnp
from jax import lax
from jax.sharding import PartitionSpec as P

WINDOW = 4096
SINKS = 4


def broadcast(x, axis, root):
    return lax.dynamic_index_in_dim(lax.all_gather(x, axis), root, 0, keepdims=False)


def shards(queries, key_heads, projected_value_heads, lengths):
    tok_rows = queries.shape[0]
    head_count = queries.shape[1]
    head_width = queries.shape[2]
    kv_heads = key_heads.shape[1]
    share = head_count // kv_heads
    position = lax.axis_index("seq")
    length_now = lengths[0]
    first_row = position * tok_rows
    score_scale = head_width ** (-0.5)
    grouped = queries.reshape(tok_rows, kv_heads, share, head_width)
    query_pos = first_row + jnp.arange(tok_rows, dtype=jnp.int32)
    last_query = first_row + tok_rows - 1

    def attend(running, kv_block, key_start, sink_mode):
        key_count = kv_block.shape[1]
        key_pos = key_start + jnp.arange(key_count, dtype=jnp.int32)
        if sink_mode:
            useful = first_row < length_now
        else:
            useful = (
                (key_start <= last_query)
                & (key_start + key_count - 1 > first_row - WINDOW)
                & (key_start < length_now)
                & (first_row < length_now)
                & (key_start + key_count > SINKS)
            )

        def compute(current):
            maximum, totals, weighted = current
            scores = (
                jnp.einsum(
                    "qhgd,khd->hgqk", grouped, kv_block[0], preferred_element_type=jnp.float32
                )
                * score_scale
            )
            distance = query_pos[:, None] - key_pos[None, :]
            if sink_mode:
                visible = (distance >= 0) & (key_pos[None, :] < length_now)
            else:
                visible = (
                    (distance >= 0)
                    & (distance < WINDOW)
                    & (key_pos[None, :] >= SINKS)
                    & (key_pos[None, :] < length_now)
                )
            visible = visible & (query_pos[:, None] < length_now)
            masked = jnp.where(visible, scores, -1e30)
            newest = jnp.maximum(maximum, jnp.max(masked, axis=-1))
            weights = jnp.where(visible, jnp.exp(scores - newest[..., None]), 0.0)
            rescale = jnp.exp(maximum - newest)
            totals = totals * rescale + jnp.sum(weights, axis=-1)
            weighted = weighted * rescale[..., None] + jnp.einsum(
                "hgqk,khd->hgqd",
                weights.astype(jnp.bfloat16),
                kv_block[1],
                preferred_element_type=jnp.float32,
            )
            return (newest, totals, weighted)

        return lax.cond(useful, compute, lambda current: current, running)

    running = (
        jnp.full((kv_heads, share, tok_rows), -1e30, jnp.float32),
        jnp.zeros((kv_heads, share, tok_rows), jnp.float32),
        jnp.zeros((kv_heads, share, tok_rows, head_width), jnp.float32),
    )
    own_pair = jnp.stack([key_heads, projected_value_heads])
    sink_pair = broadcast(own_pair[:, :SINKS], "seq", 0)
    running = attend(running, sink_pair, jnp.int32(0), True)
    shard_piece = lax.all_gather(own_pair, "seq", axis=1, tiled=True)
    piece_rows = shard_piece.shape[1]
    block_size = math.gcd(piece_rows, tok_rows)

    def one_slice(slice_index, inner):
        sliced = lax.dynamic_slice_in_dim(shard_piece, slice_index * block_size, block_size, 1)
        return attend(inner, sliced, slice_index * block_size, False)

    running = lax.fori_loop(0, piece_rows // block_size, one_slice, running)
    maximum, totals, weighted = running
    valid = query_pos < length_now
    result = jnp.where(valid[:, None], weighted / jnp.where(valid, totals, 1.0)[..., None], 0.0)
    return (
        result.transpose(2, 0, 1, 3).reshape(tok_rows, head_count, head_width).astype(jnp.bfloat16)
    )


def solution(mesh):
    in_specs = (
        P(("batch", "seq"), None, None),
        P(("batch", "seq"), None, None),
        P(("batch", "seq"), None, None),
        P("batch"),
    )
    out_specs = P(("batch", "seq"), None, None)
    return jax.shard_map(shards, mesh=mesh, in_specs=in_specs, out_specs=out_specs, check_vma=False)
```

profile of v0, /device:TPU:4, one launch (start us, length us, event | category | flops | bytes accessed | tf_op | source)
XLA Modules:
  0.0 382.0 jit_solution(8940974404311227422)
XLA Ops:
  6.5 4.4 %pad_maximum_fusion = bf16[2,512,4,256]{3,2,1,0:T(4,128)(2,1)} fusion(bf16[1,512,4,256]{3,2,1,0:T(4,128)(2,1)} %bitcast.72, bf16[1,512,4,256]{3,2,1,0:T(4,128)(2,1)} %bitcast.70), kind=kLoop, calls=%fused_computation.57 | loop fusion | flops 1048576 | bytes 4194304 | tf_op jit(solution)/shard_map/stack | solution.py:82
  14.5 24.6 %all-gather = bf16[32,4,4,256]{3,2,1,0:T(4,128)(2,1)S(1)} all-gather(bf16[2,4,4,256]{3,2,1,0:T(4,128)(2,1)S(1)} %fusion.35), channel_id=2, replica_groups=mesh['batch'=8,'seq'=16] {'seq'}, dimensions={0}, use_global_device_ids=true | all-gather | bytes 278528 | tf_op jit(solution)/shard_map/all_gather | solution.py:12
  39.1 7.7 %conditional.2 = (f32[4,2,512]{2,1,0:T(2,128)}, f32[4,2,512]{2,1,0:T(2,128)S(1)}, f32[4,2,512,256]{3,2,1,0:T(8,128)}) conditional(s32[]{:T(128)} %convert_element_type.33, () %tuple.61, (s32[512]{0:T(512)S(1)}, s32[4]{0:T(128)S(1)}, s32[]{:T(128)}, s32[4]{0:T(128)S(1)}, bf16[16,2,4,4,256]{4,3,2,1,0:T(4,128)(2,1)S(1)}, ...), branch_computations={%region_0.1_spmd, %region_1.4_spmd} | conditional | flops 17998340 | bytes 7222344 | solution.py:75
  46.8 164.4 %all-gather.3.cloned.1.call-done = bf16[2,8192,4,256]{3,2,1,0:T(4,128)(2,1)} async-done(((bf16[2,512,4,256]{3,2,1,0:T(4,128)(2,1)}), bf16[2,8192,4,256]{3,2,1,0:T(4,128)(2,1)}) %all-gather.3.cloned.1.call-update) | async-done | bytes 33554448 | tf_op jit(solution)/shard_map/all_gather | solution.py:85
  211.2 23.1 %copy.13 = bf16[2,8192,4,256]{3,1,2,0:T(8,128)(2,1)} copy(bf16[2,8192,4,256]{3,2,1,0:T(4,128)(2,1)} %all-gather.3.cloned.1.call-done) | data formatting | bytes 67108864
  234.3 135.7 %while.22 = (s32[]{:T(128)}, f32[4,2,512]{2,1,0:T(2,128)}, f32[4,2,512]{2,1,0:T(2,128)S(1)}, f32[4,2,512,256]{3,2,1,0:T(8,128)}, s32[]{:T(128)}, /*index=5*/s32[...) while((s32[]{:T(128)}, f32[4,2,512]{2,1,0:T(2,128)}, ...), condition=%wide.region_9.10_spmd.clone, body=%wide.region_4.9_spmd.clone.sunk | while | flops 2174495232 | bytes 39079348 | solution.py:93
  234.9 13.8 %conditional.5 = ((f32[4,2,512]{2,1,0:T(2,128)}, f32[4,2,512]{2,1,0:T(2,128)S(1)}, f32[4,2,512,256]{3,2,1,0:T(8,128)})) conditional(s32[]{:T(128)} %convert_element_type.46, (f32[4,2,512]{2,1,0:T(2,128)}, f32[4,2,512]{2,1,0:T(2,128)S(1)}, f32[4,2,512,256]{3,2,1,0:T(8,128)}) %tuple.89, (s32[]{:T(128)}, s32[]{:T(128)}, s32[512]{0:T(512)S(1)}, ...), branch_computations={%region_5.5_spmd, %region_6.8_spmd} | conditional | flops 2174495232 | bytes 39076968 | solution.py:75
  242.0 6.2 %multiply_add_fusion = f32[4,2,512,256]{3,2,1,0:T(8,128)} fusion(f32[4,2,512,256]{3,2,1,0:T(8,128)} %get-tuple-element.461, f32[4,2,512]{2,1,0:T(2,128)S(1)} %bitcast.74, f32[4,512,512,2]{2,1,3,0:T(8,128)S(1)} %get-tuple-element.568, f32[4,2,512]{2,1,0:T(2,128)S(1)} %max.4, pred[512,512]{0,1:T(8,128)(4,1)S(1)} %fusion.30, ...), kind=kOutput, calls=%fused_computation.30 | convolution fusion | flops 1084227584 | bytes 18120712 | tf_op jit(solution)/shard_map/while/body/eval_jaxpr/cond/branch_1_fun/hgqk,khd->hgqd/dot_general | solution.py:67
  249.5 13.8 %conditional.5 = ((f32[4,2,512]{2,1,0:T(2,128)}, f32[4,2,512]{2,1,0:T(2,128)S(1)}, f32[4,2,512,256]{3,2,1,0:T(8,128)})) conditional(s32[]{:T(128)} %convert_element_type.46, (f32[4,2,512]{2,1,0:T(2,128)}, f32[4,2,512]{2,1,0:T(2,128)S(1)}, f32[4,2,512,256]{3,2,1,0:T(8,128)}) %tuple.89, (s32[]{:T(128)}, s32[]{:T(128)}, s32[512]{0:T(512)S(1)}, ...), branch_computations={%region_5.5_spmd, %region_6.8_spmd} | conditional | flops 2174495232 | bytes 39076968 | solution.py:75
  256.5 6.2 %multiply_add_fusion = f32[4,2,512,256]{3,2,1,0:T(8,128)} fusion(f32[4,2,512,256]{3,2,1,0:T(8,128)} %get-tuple-element.461, f32[4,2,512]{2,1,0:T(2,128)S(1)} %bitcast.74, f32[4,512,512,2]{2,1,3,0:T(8,128)S(1)} %get-tuple-element.568, f32[4,2,512]{2,1,0:T(2,128)S(1)} %max.4, pred[512,512]{0,1:T(8,128)(4,1)S(1)} %fusion.30, ...), kind=kOutput, calls=%fused_computation.30 | convolution fusion | flops 1084227584 | bytes 18120712 | tf_op jit(solution)/shard_map/while/body/eval_jaxpr/cond/branch_1_fun/hgqk,khd->hgqd/dot_general | solution.py:67
  264.0 13.8 %conditional.5 = ((f32[4,2,512]{2,1,0:T(2,128)}, f32[4,2,512]{2,1,0:T(2,128)S(1)}, f32[4,2,512,256]{3,2,1,0:T(8,128)})) conditional(s32[]{:T(128)} %convert_element_type.46, (f32[4,2,512]{2,1,0:T(2,128)}, f32[4,2,512]{2,1,0:T(2,128)S(1)}, f32[4,2,512,256]{3,2,1,0:T(8,128)}) %tuple.89, (s32[]{:T(128)}, s32[]{:T(128)}, s32[512]{0:T(512)S(1)}, ...), branch_computations={%region_5.5_spmd, %region_6.8_spmd} | conditional | flops 2174495232 | bytes 39076968 | solution.py:75
  271.1 6.2 %multiply_add_fusion = f32[4,2,512,256]{3,2,1,0:T(8,128)} fusion(f32[4,2,512,256]{3,2,1,0:T(8,128)} %get-tuple-element.461, f32[4,2,512]{2,1,0:T(2,128)S(1)} %bitcast.74, f32[4,512,512,2]{2,1,3,0:T(8,128)S(1)} %get-tuple-element.568, f32[4,2,512]{2,1,0:T(2,128)S(1)} %max.4, pred[512,512]{0,1:T(8,128)(4,1)S(1)} %fusion.30, ...), kind=kOutput, calls=%fused_computation.30 | convolution fusion | flops 1084227584 | bytes 18120712 | tf_op jit(solution)/shard_map/while/body/eval_jaxpr/cond/branch_1_fun/hgqk,khd->hgqd/dot_general | solution.py:67
  278.5 13.8 %conditional.5 = ((f32[4,2,512]{2,1,0:T(2,128)}, f32[4,2,512]{2,1,0:T(2,128)S(1)}, f32[4,2,512,256]{3,2,1,0:T(8,128)})) conditional(s32[]{:T(128)} %convert_element_type.46, (f32[4,2,512]{2,1,0:T(2,128)}, f32[4,2,512]{2,1,0:T(2,128)S(1)}, f32[4,2,512,256]{3,2,1,0:T(8,128)}) %tuple.89, (s32[]{:T(128)}, s32[]{:T(128)}, s32[512]{0:T(512)S(1)}, ...), branch_computations={%region_5.5_spmd, %region_6.8_spmd} | conditional | flops 2174495232 | bytes 39076968 | solution.py:75
  285.6 6.2 %multiply_add_fusion = f32[4,2,512,256]{3,2,1,0:T(8,128)} fusion(f32[4,2,512,256]{3,2,1,0:T(8,128)} %get-tuple-element.461, f32[4,2,512]{2,1,0:T(2,128)S(1)} %bitcast.74, f32[4,512,512,2]{2,1,3,0:T(8,128)S(1)} %get-tuple-element.568, f32[4,2,512]{2,1,0:T(2,128)S(1)} %max.4, pred[512,512]{0,1:T(8,128)(4,1)S(1)} %fusion.30, ...), kind=kOutput, calls=%fused_computation.30 | convolution fusion | flops 1084227584 | bytes 18120712 | tf_op jit(solution)/shard_map/while/body/eval_jaxpr/cond/branch_1_fun/hgqk,khd->hgqd/dot_general | solution.py:67
  293.0 13.8 %conditional.5 = ((f32[4,2,512]{2,1,0:T(2,128)}, f32[4,2,512]{2,1,0:T(2,128)S(1)}, f32[4,2,512,256]{3,2,1,0:T(8,128)})) conditional(s32[]{:T(128)} %convert_element_type.46, (f32[4,2,512]{2,1,0:T(2,128)}, f32[4,2,512]{2,1,0:T(2,128)S(1)}, f32[4,2,512,256]{3,2,1,0:T(8,128)}) %tuple.89, (s32[]{:T(128)}, s32[]{:T(128)}, s32[512]{0:T(512)S(1)}, ...), branch_computations={%region_5.5_spmd, %region_6.8_spmd} | conditional | flops 2174495232 | bytes 39076968 | solution.py:75
  300.1 6.2 %multiply_add_fusion = f32[4,2,512,256]{3,2,1,0:T(8,128)} fusion(f32[4,2,512,256]{3,2,1,0:T(8,128)} %get-tuple-element.461, f32[4,2,512]{2,1,0:T(2,128)S(1)} %bitcast.74, f32[4,512,512,2]{2,1,3,0:T(8,128)S(1)} %get-tuple-element.568, f32[4,2,512]{2,1,0:T(2,128)S(1)} %max.4, pred[512,512]{0,1:T(8,128)(4,1)S(1)} %fusion.30, ...), kind=kOutput, calls=%fused_computation.30 | convolution fusion | flops 1084227584 | bytes 18120712 | tf_op jit(solution)/shard_map/while/body/eval_jaxpr/cond/branch_1_fun/hgqk,khd->hgqd/dot_general | solution.py:67
  307.5 13.8 %conditional.5 = ((f32[4,2,512]{2,1,0:T(2,128)}, f32[4,2,512]{2,1,0:T(2,128)S(1)}, f32[4,2,512,256]{3,2,1,0:T(8,128)})) conditional(s32[]{:T(128)} %convert_element_type.46, (f32[4,2,512]{2,1,0:T(2,128)}, f32[4,2,512]{2,1,0:T(2,128)S(1)}, f32[4,2,512,256]{3,2,1,0:T(8,128)}) %tuple.89, (s32[]{:T(128)}, s32[]{:T(128)}, s32[512]{0:T(512)S(1)}, ...), branch_computations={%region_5.5_spmd, %region_6.8_spmd} | conditional | flops 2174495232 | bytes 39076968 | solution.py:75
  314.6 6.2 %multiply_add_fusion = f32[4,2,512,256]{3,2,1,0:T(8,128)} fusion(f32[4,2,512,256]{3,2,1,0:T(8,128)} %get-tuple-element.461, f32[4,2,512]{2,1,0:T(2,128)S(1)} %bitcast.74, f32[4,512,512,2]{2,1,3,0:T(8,128)S(1)} %get-tuple-element.568, f32[4,2,512]{2,1,0:T(2,128)S(1)} %max.4, pred[512,512]{0,1:T(8,128)(4,1)S(1)} %fusion.30, ...), kind=kOutput, calls=%fused_computation.30 | convolution fusion | flops 1084227584 | bytes 18120712 | tf_op jit(solution)/shard_map/while/body/eval_jaxpr/cond/branch_1_fun/hgqk,khd->hgqd/dot_general | solution.py:67
  322.0 13.8 %conditional.5 = ((f32[4,2,512]{2,1,0:T(2,128)}, f32[4,2,512]{2,1,0:T(2,128)S(1)}, f32[4,2,512,256]{3,2,1,0:T(8,128)})) conditional(s32[]{:T(128)} %convert_element_type.46, (f32[4,2,512]{2,1,0:T(2,128)}, f32[4,2,512]{2,1,0:T(2,128)S(1)}, f32[4,2,512,256]{3,2,1,0:T(8,128)}) %tuple.89, (s32[]{:T(128)}, s32[]{:T(128)}, s32[512]{0:T(512)S(1)}, ...), branch_computations={%region_5.5_spmd, %region_6.8_spmd} | conditional | flops 2174495232 | bytes 39076968 | solution.py:75
  329.1 6.2 %multiply_add_fusion = f32[4,2,512,256]{3,2,1,0:T(8,128)} fusion(f32[4,2,512,256]{3,2,1,0:T(8,128)} %get-tuple-element.461, f32[4,2,512]{2,1,0:T(2,128)S(1)} %bitcast.74, f32[4,512,512,2]{2,1,3,0:T(8,128)S(1)} %get-tuple-element.568, f32[4,2,512]{2,1,0:T(2,128)S(1)} %max.4, pred[512,512]{0,1:T(8,128)(4,1)S(1)} %fusion.30, ...), kind=kOutput, calls=%fused_computation.30 | convolution fusion | flops 1084227584 | bytes 18120712 | tf_op jit(solution)/shard_map/while/body/eval_jaxpr/cond/branch_1_fun/hgqk,khd->hgqd/dot_general | solution.py:67
  336.6 13.8 %conditional.5 = ((f32[4,2,512]{2,1,0:T(2,128)}, f32[4,2,512]{2,1,0:T(2,128)S(1)}, f32[4,2,512,256]{3,2,1,0:T(8,128)})) conditional(s32[]{:T(128)} %convert_element_type.46, (f32[4,2,512]{2,1,0:T(2,128)}, f32[4,2,512]{2,1,0:T(2,128)S(1)}, f32[4,2,512,256]{3,2,1,0:T(8,128)}) %tuple.89, (s32[]{:T(128)}, s32[]{:T(128)}, s32[512]{0:T(512)S(1)}, ...), branch_computations={%region_5.5_spmd, %region_6.8_spmd} | conditional | flops 2174495232 | bytes 39076968 | solution.py:75
  343.7 6.2 %multiply_add_fusion = f32[4,2,512,256]{3,2,1,0:T(8,128)} fusion(f32[4,2,512,256]{3,2,1,0:T(8,128)} %get-tuple-element.461, f32[4,2,512]{2,1,0:T(2,128)S(1)} %bitcast.74, f32[4,512,512,2]{2,1,3,0:T(8,128)S(1)} %get-tuple-element.568, f32[4,2,512]{2,1,0:T(2,128)S(1)} %max.4, pred[512,512]{0,1:T(8,128)(4,1)S(1)} %fusion.30, ...), kind=kOutput, calls=%fused_computation.30 | convolution fusion | flops 1084227584 | bytes 18120712 | tf_op jit(solution)/shard_map/while/body/eval_jaxpr/cond/branch_1_fun/hgqk,khd->hgqd/dot_general | solution.py:67
  351.1 13.8 %conditional.5 = ((f32[4,2,512]{2,1,0:T(2,128)}, f32[4,2,512]{2,1,0:T(2,128)S(1)}, f32[4,2,512,256]{3,2,1,0:T(8,128)})) conditional(s32[]{:T(128)} %convert_element_type.46, (f32[4,2,512]{2,1,0:T(2,128)}, f32[4,2,512]{2,1,0:T(2,128)S(1)}, f32[4,2,512,256]{3,2,1,0:T(8,128)}) %tuple.89, (s32[]{:T(128)}, s32[]{:T(128)}, s32[512]{0:T(512)S(1)}, ...), branch_computations={%region_5.5_spmd, %region_6.8_spmd} | conditional | flops 2174495232 | bytes 39076968 | solution.py:75
  358.2 6.2 %multiply_add_fusion = f32[4,2,512,256]{3,2,1,0:T(8,128)} fusion(f32[4,2,512,256]{3,2,1,0:T(8,128)} %get-tuple-element.461, f32[4,2,512]{2,1,0:T(2,128)S(1)} %bitcast.74, f32[4,512,512,2]{2,1,3,0:T(8,128)S(1)} %get-tuple-element.568, f32[4,2,512]{2,1,0:T(2,128)S(1)} %max.4, pred[512,512]{0,1:T(8,128)(4,1)S(1)} %fusion.30, ...), kind=kOutput, calls=%fused_computation.30 | convolution fusion | flops 1084227584 | bytes 18120712 | tf_op jit(solution)/shard_map/while/body/eval_jaxpr/cond/branch_1_fun/hgqk,khd->hgqd/dot_general | solution.py:67
  (116 shorter events, 84.4 us)
Async XLA Ops:
  6.5 204.7 %all-gather.3.cloned.1.call-start = ((), (), s32[]{:S(2)}) async-start(), calls=%async_computation | async-start | bytes 35651584 | tf_op jit(solution)/shard_map/all_gather | solution.py:85
  11.0 2.8 copy-start
Sparse Core Ops, SparseCore 0:
  11.1 200.0 all-gather.2
where the time goes:
time: 384 us; the launch traced here: 382 us
  waiting for transfers between devices  164 us (43%)
  matrix products  84.2 us (22%)
  other arithmetic  49.8 us (13%)
  local copies, waits for them, and re-layouts  33.1 us (9%)
  blocking collectives  24.6 us (6%)
  between operations  14.2 us (4%)
  loops' own time  11.7 us (3%)
    all_gather x1, waiting for transfers between devices, shards(): shard_piece = lax.all_gather(own_pair, 'seq', axis=1, tiled=True)  164 us
    dot_general x10, matrix products, compute(): jnp.einsum('hgqk,khd->hgqd', weights.astype(jnp.bfloat16), kv_block[1], p...  58.7 us
    dot_general x10, matrix products, compute(): jnp.einsum('qhgd,khd->hgqk', grouped, kv_block[0], preferred_element_type...  25.5 us
    unnamed x4, local copies, waits for them, and re-layouts  25.1 us
    all_gather x1, blocking collectives, broadcast(): lax.all_gather(x, axis)  24.6 us
    reduce_sum x10, other arithmetic, compute(): totals = totals * rescale + jnp.sum(weights, axis=-1)  16.4 us
    another operation x1, loops' own time, shards(): running = lax.fori_loop(0, piece_rows // block_size, one_slice, running)  10.9 us
  transfers between devices with their start and end apart: 1, of which 1 were waited for; matrix products, arithmetic and copies ran while one was open for 3% of the time, Pallas kernels for 0%

commit v1 on v0

--- a/solution.py
+++ b/solution.py
@@ -82,7 +82,9 @@
     own_pair = jnp.stack([key_heads, projected_value_heads])
     sink_pair = broadcast(own_pair[:, :SINKS], "seq", 0)
     running = attend(running, sink_pair, jnp.int32(0), True)
-    shard_piece = lax.all_gather(own_pair, "seq", axis=1, tiled=True)
+    shard_piece = jnp.concatenate(
+        lax.all_to_all(jnp.stack([own_pair] * lax.axis_size("seq")), "seq", 0, 0), axis=1
+    )
     piece_rows = shard_piece.shape[1]
     block_size = math.gcd(piece_rows, tok_rows)
 

time: 384 us -> 871 us (2.27)
  blocking collectives: 24.6 us -> 634 us
  waiting for transfers between devices: 164 us -> 0.01 us
  matrix products: 84.2 us -> 114 us
  local copies, waits for them, and re-layouts: 33.1 us -> 50.5 us
  between operations: 14.2 us -> 0.75 us
    all_gather x1, blocking collectives: 24.6 us -> 634 us  [broadcast(): lax.all_gather(x, axis)]
    all_gather x1 -> x0, waiting for transfers between devices: 164 us -> none  [shards(): shard_piece = lax.all_gather(own_pair, 'seq', axis=1, tiled=True)]
    dot_general x10, matrix products: 58.7 us -> 88.3 us  [compute(): jnp.einsum('hgqk,khd->hgqd', weights.astype(jnp.bfloat16), kv_block[1], p...]
    unnamed x4 -> x3, local copies, waits for them, and re-layouts: 25.1 us -> 2.11 us
    all_to_all x0 -> x1, local copies, waits for them, and re-layouts: none -> 22.9 us  [shards(): lax.all_to_all(jnp.stack([own_pair] * lax.axis_size('seq')), 'seq', 0, 0)]
    another operation x1 -> x3, local copies, waits for them, and re-layouts: 0.12 us -> 11.4 us  [the longest x1 11 us: shards(): jnp.stack([own_pair] * lax.axis_size('seq'))]
  transfers between devices with their start and end apart: 1 -> 1, of which waited for: 1 -> 0; matrix products, arithmetic and copies ran while one was open for 3% -> 1% of each run, Pallas kernels for 0% -> 0%
where the time goes in v1:
time: 871 us; the launch traced here: 867 us
  blocking collectives  634 us (73%)
  matrix products  114 us (13%)
  local copies, waits for them, and re-layouts  50.5 us (6%)
  other arithmetic  48.9 us (6%)
  loops' own time  11.9 us (1%)
    all_gather x1, blocking collectives, broadcast(): lax.all_gather(x, axis)  634 us
    dot_general x10, matrix products, compute(): jnp.einsum('hgqk,khd->hgqd', weights.astype(jnp.bfloat16), kv_block[1], p...  88.3 us
    dot_general x10, matrix products, compute(): jnp.einsum('qhgd,khd->hgqk', grouped, kv_block[0], preferred_element_type...  25.4 us
    all_to_all x1, local copies, waits for them, and re-layouts, shards(): lax.all_to_all(jnp.stack([own_pair] * lax.axis_size('seq')), 'seq', 0, 0)  22.9 us
  transfers between devices with their start and end apart: 1, of which 0 were waited for; matrix products, arithmetic and copies ran while one was open for 1% of the time, Pallas kernels for 0%

profile of v1, /device:TPU:4, one launch (start us, length us, event | category | flops | bytes accessed | tf_op | source)
XLA Modules:
  0.0 867.1 jit_solution(4571570694009640507)
XLA Ops:
  3.4 11.0 %stack.11 = bf16[16,2,512,4,256]{4,2,3,1,0:T(8,128)(2,1)} broadcast(bf16[2,512,4,256]{3,1,2,0:T(8,128)(2,1)S(1)} %copy.18), dimensions={1,2,3,4} | broadcast | bytes 35651584 | tf_op jit(solution)/shard_map/stack | solution.py:86
  14.4 7.5 all-to-all-start
  25.4 633.8 %all-gather = bf16[32,4,4,256]{3,2,1,0:T(4,128)(2,1)S(1)} all-gather(bf16[2,4,4,256]{3,2,1,0:T(4,128)(2,1)S(1)} %fusion.35), channel_id=2, replica_groups=mesh['batch'=8,'seq'=16] {'seq'}, dimensions={0}, use_global_device_ids=true | all-gather | bytes 278528 | tf_op jit(solution)/shard_map/all_gather | solution.py:12
  659.2 7.8 conditional.2
  666.9 22.9 %copy.19 = bf16[16,2,512,4,256]{4,2,0,3,1:T(8,128)(2,1)} copy(bf16[16,2,512,4,256]{4,2,3,1,0:T(8,128)(2,1)} %all-to-all-done) | data formatting | bytes 67108864 | tf_op jit(solution)/shard_map/all_to_all | solution.py:86
  689.8 172.1 %while.22 = (s32[]{:T(128)}, f32[4,2,512]{2,1,0:T(2,128)}, f32[4,2,512]{2,1,0:T(2,128)S(1)}, f32[4,2,512,256]{3,2,1,0:T(8,128)}, s32[]{:T(128)}, /*index=5*/s32[...) while((s32[]{:T(128)}, f32[4,2,512]{2,1,0:T(2,128)}, ...), condition=%wide.region_9.10_spmd.clone, body=%wide.region_4.9_spmd.clone.sunk | while | flops 2174495232 | bytes 72633808 | solution.py:95
  690.5 17.9 %conditional.5 = ((f32[4,2,512]{2,1,0:T(2,128)}, f32[4,2,512]{2,1,0:T(2,128)S(1)}, f32[4,2,512,256]{3,2,1,0:T(8,128)})) conditional(s32[]{:T(128)} %convert_element_type.46, (f32[4,2,512]{2,1,0:T(2,128)}, f32[4,2,512]{2,1,0:T(2,128)S(1)}, f32[4,2,512,256]{3,2,1,0:T(8,128)}) %tuple.89, (s32[]{:T(128)}, s32[]{:T(128)}, s32[512]{0:T(512)S(1)}, ...), branch_computations={%region_5.5_spmd, %region_6.8_spmd} | conditional | flops 2174495232 | bytes 72631424 | solution.py:75
  698.3 9.5 %multiply_add_fusion = f32[4,2,512,256]{3,2,1,0:T(8,128)} fusion(f32[4,2,512,256]{3,2,1,0:T(8,128)} %get-tuple-element.461, f32[4,2,512]{2,1,0:T(2,128)S(1)} %bitcast.78, f32[4,512,512,2]{2,1,3,0:T(8,128)} %copy-done, f32[4,2,512]{2,1,0:T(2,128)S(1)} %max.4, pred[512,512]{0,1:T(8,128)(4,1)S(1)} %fusion.30, ...), kind=kOutput, calls=%fused_computation.30 | convolution fusion | flops 1084227584 | bytes 18120712 | tf_op jit(solution)/shard_map/while/body/eval_jaxpr/cond/branch_1_fun/hgqk,khd->hgqd/dot_general | solution.py:67
  709.1 17.9 %conditional.5 = ((f32[4,2,512]{2,1,0:T(2,128)}, f32[4,2,512]{2,1,0:T(2,128)S(1)}, f32[4,2,512,256]{3,2,1,0:T(8,128)})) conditional(s32[]{:T(128)} %convert_element_type.46, (f32[4,2,512]{2,1,0:T(2,128)}, f32[4,2,512]{2,1,0:T(2,128)S(1)}, f32[4,2,512,256]{3,2,1,0:T(8,128)}) %tuple.89, (s32[]{:T(128)}, s32[]{:T(128)}, s32[512]{0:T(512)S(1)}, ...), branch_computations={%region_5.5_spmd, %region_6.8_spmd} | conditional | flops 2174495232 | bytes 72631424 | solution.py:75
  716.9 9.5 %multiply_add_fusion = f32[4,2,512,256]{3,2,1,0:T(8,128)} fusion(f32[4,2,512,256]{3,2,1,0:T(8,128)} %get-tuple-element.461, f32[4,2,512]{2,1,0:T(2,128)S(1)} %bitcast.78, f32[4,512,512,2]{2,1,3,0:T(8,128)} %copy-done, f32[4,2,512]{2,1,0:T(2,128)S(1)} %max.4, pred[512,512]{0,1:T(8,128)(4,1)S(1)} %fusion.30, ...), kind=kOutput, calls=%fused_computation.30 | convolution fusion | flops 1084227584 | bytes 18120712 | tf_op jit(solution)/shard_map/while/body/eval_jaxpr/cond/branch_1_fun/hgqk,khd->hgqd/dot_general | solution.py:67
  727.6 17.9 %conditional.5 = ((f32[4,2,512]{2,1,0:T(2,128)}, f32[4,2,512]{2,1,0:T(2,128)S(1)}, f32[4,2,512,256]{3,2,1,0:T(8,128)})) conditional(s32[]{:T(128)} %convert_element_type.46, (f32[4,2,512]{2,1,0:T(2,128)}, f32[4,2,512]{2,1,0:T(2,128)S(1)}, f32[4,2,512,256]{3,2,1,0:T(8,128)}) %tuple.89, (s32[]{:T(128)}, s32[]{:T(128)}, s32[512]{0:T(512)S(1)}, ...), branch_computations={%region_5.5_spmd, %region_6.8_spmd} | conditional | flops 2174495232 | bytes 72631424 | solution.py:75
  735.4 9.5 %multiply_add_fusion = f32[4,2,512,256]{3,2,1,0:T(8,128)} fusion(f32[4,2,512,256]{3,2,1,0:T(8,128)} %get-tuple-element.461, f32[4,2,512]{2,1,0:T(2,128)S(1)} %bitcast.78, f32[4,512,512,2]{2,1,3,0:T(8,128)} %copy-done, f32[4,2,512]{2,1,0:T(2,128)S(1)} %max.4, pred[512,512]{0,1:T(8,128)(4,1)S(1)} %fusion.30, ...), kind=kOutput, calls=%fused_computation.30 | convolution fusion | flops 1084227584 | bytes 18120712 | tf_op jit(solution)/shard_map/while/body/eval_jaxpr/cond/branch_1_fun/hgqk,khd->hgqd/dot_general | solution.py:67
  746.2 17.9 %conditional.5 = ((f32[4,2,512]{2,1,0:T(2,128)}, f32[4,2,512]{2,1,0:T(2,128)S(1)}, f32[4,2,512,256]{3,2,1,0:T(8,128)})) conditional(s32[]{:T(128)} %convert_element_type.46, (f32[4,2,512]{2,1,0:T(2,128)}, f32[4,2,512]{2,1,0:T(2,128)S(1)}, f32[4,2,512,256]{3,2,1,0:T(8,128)}) %tuple.89, (s32[]{:T(128)}, s32[]{:T(128)}, s32[512]{0:T(512)S(1)}, ...), branch_computations={%region_5.5_spmd, %region_6.8_spmd} | conditional | flops 2174495232 | bytes 72631424 | solution.py:75
  754.0 9.5 %multiply_add_fusion = f32[4,2,512,256]{3,2,1,0:T(8,128)} fusion(f32[4,2,512,256]{3,2,1,0:T(8,128)} %get-tuple-element.461, f32[4,2,512]{2,1,0:T(2,128)S(1)} %bitcast.78, f32[4,512,512,2]{2,1,3,0:T(8,128)} %copy-done, f32[4,2,512]{2,1,0:T(2,128)S(1)} %max.4, pred[512,512]{0,1:T(8,128)(4,1)S(1)} %fusion.30, ...), kind=kOutput, calls=%fused_computation.30 | convolution fusion | flops 1084227584 | bytes 18120712 | tf_op jit(solution)/shard_map/while/body/eval_jaxpr/cond/branch_1_fun/hgqk,khd->hgqd/dot_general | solution.py:67
  764.7 17.9 %conditional.5 = ((f32[4,2,512]{2,1,0:T(2,128)}, f32[4,2,512]{2,1,0:T(2,128)S(1)}, f32[4,2,512,256]{3,2,1,0:T(8,128)})) conditional(s32[]{:T(128)} %convert_element_type.46, (f32[4,2,512]{2,1,0:T(2,128)}, f32[4,2,512]{2,1,0:T(2,128)S(1)}, f32[4,2,512,256]{3,2,1,0:T(8,128)}) %tuple.89, (s32[]{:T(128)}, s32[]{:T(128)}, s32[512]{0:T(512)S(1)}, ...), branch_computations={%region_5.5_spmd, %region_6.8_spmd} | conditional | flops 2174495232 | bytes 72631424 | solution.py:75
  772.5 9.5 %multiply_add_fusion = f32[4,2,512,256]{3,2,1,0:T(8,128)} fusion(f32[4,2,512,256]{3,2,1,0:T(8,128)} %get-tuple-element.461, f32[4,2,512]{2,1,0:T(2,128)S(1)} %bitcast.78, f32[4,512,512,2]{2,1,3,0:T(8,128)} %copy-done, f32[4,2,512]{2,1,0:T(2,128)S(1)} %max.4, pred[512,512]{0,1:T(8,128)(4,1)S(1)} %fusion.30, ...), kind=kOutput, calls=%fused_computation.30 | convolution fusion | flops 1084227584 | bytes 18120712 | tf_op jit(solution)/shard_map/while/body/eval_jaxpr/cond/branch_1_fun/hgqk,khd->hgqd/dot_general | solution.py:67
  783.3 17.9 %conditional.5 = ((f32[4,2,512]{2,1,0:T(2,128)}, f32[4,2,512]{2,1,0:T(2,128)S(1)}, f32[4,2,512,256]{3,2,1,0:T(8,128)})) conditional(s32[]{:T(128)} %convert_element_type.46, (f32[4,2,512]{2,1,0:T(2,128)}, f32[4,2,512]{2,1,0:T(2,128)S(1)}, f32[4,2,512,256]{3,2,1,0:T(8,128)}) %tuple.89, (s32[]{:T(128)}, s32[]{:T(128)}, s32[512]{0:T(512)S(1)}, ...), branch_computations={%region_5.5_spmd, %region_6.8_spmd} | conditional | flops 2174495232 | bytes 72631424 | solution.py:75
  791.1 9.5 %multiply_add_fusion = f32[4,2,512,256]{3,2,1,0:T(8,128)} fusion(f32[4,2,512,256]{3,2,1,0:T(8,128)} %get-tuple-element.461, f32[4,2,512]{2,1,0:T(2,128)S(1)} %bitcast.78, f32[4,512,512,2]{2,1,3,0:T(8,128)} %copy-done, f32[4,2,512]{2,1,0:T(2,128)S(1)} %max.4, pred[512,512]{0,1:T(8,128)(4,1)S(1)} %fusion.30, ...), kind=kOutput, calls=%fused_computation.30 | convolution fusion | flops 1084227584 | bytes 18120712 | tf_op jit(solution)/shard_map/while/body/eval_jaxpr/cond/branch_1_fun/hgqk,khd->hgqd/dot_general | solution.py:67
  801.8 17.9 %conditional.5 = ((f32[4,2,512]{2,1,0:T(2,128)}, f32[4,2,512]{2,1,0:T(2,128)S(1)}, f32[4,2,512,256]{3,2,1,0:T(8,128)})) conditional(s32[]{:T(128)} %convert_element_type.46, (f32[4,2,512]{2,1,0:T(2,128)}, f32[4,2,512]{2,1,0:T(2,128)S(1)}, f32[4,2,512,256]{3,2,1,0:T(8,128)}) %tuple.89, (s32[]{:T(128)}, s32[]{:T(128)}, s32[512]{0:T(512)S(1)}, ...), branch_computations={%region_5.5_spmd, %region_6.8_spmd} | conditional | flops 2174495232 | bytes 72631424 | solution.py:75
  809.7 9.5 %multiply_add_fusion = f32[4,2,512,256]{3,2,1,0:T(8,128)} fusion(f32[4,2,512,256]{3,2,1,0:T(8,128)} %get-tuple-element.461, f32[4,2,512]{2,1,0:T(2,128)S(1)} %bitcast.78, f32[4,512,512,2]{2,1,3,0:T(8,128)} %copy-done, f32[4,2,512]{2,1,0:T(2,128)S(1)} %max.4, pred[512,512]{0,1:T(8,128)(4,1)S(1)} %fusion.30, ...), kind=kOutput, calls=%fused_computation.30 | convolution fusion | flops 1084227584 | bytes 18120712 | tf_op jit(solution)/shard_map/while/body/eval_jaxpr/cond/branch_1_fun/hgqk,khd->hgqd/dot_general | solution.py:67
  820.4 17.9 %conditional.5 = ((f32[4,2,512]{2,1,0:T(2,128)}, f32[4,2,512]{2,1,0:T(2,128)S(1)}, f32[4,2,512,256]{3,2,1,0:T(8,128)})) conditional(s32[]{:T(128)} %convert_element_type.46, (f32[4,2,512]{2,1,0:T(2,128)}, f32[4,2,512]{2,1,0:T(2,128)S(1)}, f32[4,2,512,256]{3,2,1,0:T(8,128)}) %tuple.89, (s32[]{:T(128)}, s32[]{:T(128)}, s32[512]{0:T(512)S(1)}, ...), branch_computations={%region_5.5_spmd, %region_6.8_spmd} | conditional | flops 2174495232 | bytes 72631424 | solution.py:75
  828.2 9.5 %multiply_add_fusion = f32[4,2,512,256]{3,2,1,0:T(8,128)} fusion(f32[4,2,512,256]{3,2,1,0:T(8,128)} %get-tuple-element.461, f32[4,2,512]{2,1,0:T(2,128)S(1)} %bitcast.78, f32[4,512,512,2]{2,1,3,0:T(8,128)} %copy-done, f32[4,2,512]{2,1,0:T(2,128)S(1)} %max.4, pred[512,512]{0,1:T(8,128)(4,1)S(1)} %fusion.30, ...), kind=kOutput, calls=%fused_computation.30 | convolution fusion | flops 1084227584 | bytes 18120712 | tf_op jit(solution)/shard_map/while/body/eval_jaxpr/cond/branch_1_fun/hgqk,khd->hgqd/dot_general | solution.py:67
  839.0 17.9 %conditional.5 = ((f32[4,2,512]{2,1,0:T(2,128)}, f32[4,2,512]{2,1,0:T(2,128)S(1)}, f32[4,2,512,256]{3,2,1,0:T(8,128)})) conditional(s32[]{:T(128)} %convert_element_type.46, (f32[4,2,512]{2,1,0:T(2,128)}, f32[4,2,512]{2,1,0:T(2,128)S(1)}, f32[4,2,512,256]{3,2,1,0:T(8,128)}) %tuple.89, (s32[]{:T(128)}, s32[]{:T(128)}, s32[512]{0:T(512)S(1)}, ...), branch_computations={%region_5.5_spmd, %region_6.8_spmd} | conditional | flops 2174495232 | bytes 72631424 | solution.py:75
  846.8 9.5 %multiply_add_fusion = f32[4,2,512,256]{3,2,1,0:T(8,128)} fusion(f32[4,2,512,256]{3,2,1,0:T(8,128)} %get-tuple-element.461, f32[4,2,512]{2,1,0:T(2,128)S(1)} %bitcast.78, f32[4,512,512,2]{2,1,3,0:T(8,128)} %copy-done, f32[4,2,512]{2,1,0:T(2,128)S(1)} %max.4, pred[512,512]{0,1:T(8,128)(4,1)S(1)} %fusion.30, ...), kind=kOutput, calls=%fused_computation.30 | convolution fusion | flops 1084227584 | bytes 18120712 | tf_op jit(solution)/shard_map/while/body/eval_jaxpr/cond/branch_1_fun/hgqk,khd->hgqd/dot_general | solution.py:67
  (135 shorter events, 94.3 us)
Async XLA Ops:
  14.4 652.5 %all-to-all-start = ((bf16[16,2,512,4,256]{4,2,3,1,0:T(8,128)(2,1)}), bf16[16,2,512,4,256]{4,2,3,1,0:T(8,128)(2,1)}, u32[]{:S(2)}, u32[]{:S(2)}) async-start(bf16[16,2,512,4,256]{4,2,3,1,0:T(8,128)(2,1)} %stack.11), calls=%async_computation | async-start | bytes 67108864 | tf_op jit(solution)/shard_map/all_to_all | solution.py:86
  21.9 2.8 copy-start.1
  694.4 3.2 copy-start
  712.9 3.2 copy-start
  731.5 3.2 copy-start
  750.1 3.2 copy-start
  768.6 3.2 copy-start
  787.2 3.2 copy-start
  805.7 3.2 copy-start
  824.3 3.2 copy-start
  842.9 3.2 copy-start
